TPU v7x, 256 devices: a 8x8x2 block of a 8x8x16 slice. The times are simulated.
256 devices in a mesh: groups: 2 (over z), ep: 128 (over y, x, core).
Axes of the slice: x: 8, y: 8, z: 2, core: 2. Of those that a mesh axis runs over, the one named last changes fastest.
The devices are a block of a 8x8x16 slice.
Arguments:
- tokens: bfloat16 [2048, 7168], P(('groups', 'ep')), parts along dimension 0, may hold values from -6 to 6
- experts: int32 [2048, 8], P(('groups', 'ep')), parts along dimension 0, may hold values from 0 to 15, as said below
- gate_fixed: int32 [2048, 8], P(('groups', 'ep')), parts along dimension 0, may hold values from 1 to 65535
- home_slot: int32 [2048], P(('groups', 'ep')), parts along dimension 0, may hold values from 0 to 7, as said below
- bias: float32 [16], replicated, may hold values from -0.5 to 0.5
- w_gate: bfloat16 [7168, 32768], P(None, 'ep'), may hold values from -0.0625 to 0.0625
- w_up: bfloat16 [7168, 32768], P(None, 'ep'), may hold values from -0.0625 to 0.0625
- w_down: bfloat16 [32768, 7168], P('ep'), may hold values from -0.125 to 0.125
Outputs:
- moe_out: bfloat16 [2048, 7168], P(('groups', 'ep')), parts along dimension 0
- bias_next: float32 [32], P('groups'), parts along dimension 0
There are 2 independent parts, one for each index of `groups`. A program takes and returns all parts, laid end to end along the dimension named above; an argument that names none is the same for every part. Nothing has to cross between parts.
Inputs may be any that keep to these rules, and one draw needn't show every extreme that they name: Each token names 8 different experts; among the tokens of one device no expert is named more than 6 times, and some device reaches that bound. `home_slot`: within each device's block of 8 tokens every value appears exactly once.
All inputs are finite; a program needn't handle non-finite values.
Results may differ from a plain program's by a relative error of at most 0.008.
Values may be sent and summed in bfloat16 or wider, within the bound.
A program may use at most 128 MiB of HBM per device.

v0:
```python
import math

import jax
import jax.numpy as jnp
from jax import lax
from jax.sharding import PartitionSpec as P

ROUTED_SCALE = 2.5


def in_one_piece(arrays, axis, dim, along):
    ends, at = ([], 0)
    for a in arrays[:-1]:
        at += a.shape[along]
        ends.append(at)
    both = jnp.concatenate(arrays, axis=along)
    return tuple(jnp.split(lax.all_gather(both, axis, axis=dim, tiled=True), ends, axis=along))


def in_blocks(array, dim, devices):
    before, after = (array.shape[:dim], array.shape[dim + 1 :])
    return jnp.moveaxis(array.reshape(*before, devices, -1, *after), dim, 0)


def cut_rows(length, count):
    unit = 8 if length >= 8 * count else 1
    return [length // unit * k // count * unit for k in range(1, count)]


def in_order(tiles, dim):
    tiles = jnp.moveaxis(tiles, 0, dim)
    lengths = tiles.shape
    return tiles.reshape(*lengths[:dim], lengths[dim] * lengths[dim + 1], *lengths[dim + 2 :])


def several_exchanges(array, axis, pieces, split_dim, concat_dim):
    tiles = in_blocks(array, split_dim, lax.axis_size(axis))
    cut = max(range(1, max(2, tiles.ndim - 1)), key=lambda d: tiles.shape[d])
    outs = []
    for piece in jnp.split(tiles, cut_rows(tiles.shape[cut], pieces), axis=cut):
        if piece.size:
            outs.append(lax.all_to_all(piece, axis, split_axis=0, concat_axis=0, tiled=True))
    return in_order(jnp.concatenate(outs, axis=cut), concat_dim)


def gathered_total(array, axis):
    tiles = lax.all_gather(array, axis)
    return tiles.sum(axis=0)


def expert_rows(row_block, w_gate, w_up, w_down):
    gate_part = jnp.dot(row_block, w_gate, preferred_element_type=jnp.float32)
    up_part = jnp.dot(row_block, w_up, preferred_element_type=jnp.float32)
    hidden = (jax.nn.silu(gate_part) * up_part).astype(jnp.bfloat16)
    return jnp.dot(hidden, w_down, preferred_element_type=jnp.float32).astype(jnp.bfloat16)


def per_device(tokens, experts, gate_fixed, home_slot, bias, w_gate, w_up, w_down):
    tok_rows, model_width = tokens.shape
    top_count = experts.shape[1]
    expert_count = bias.shape[0]
    device_count = lax.axis_size("ep")
    shards = device_count // expert_count
    capacity = max(
        2, min(tok_rows, (3 * tok_rows * top_count + 2 * expert_count - 1) // (2 * expert_count))
    )
    pair_count = tok_rows * top_count
    flat_ids = experts.reshape(pair_count)
    hit_table = (flat_ids[:, None] == jnp.arange(expert_count, dtype=jnp.int32)[None, :]).astype(
        jnp.int32
    )
    earlier = jnp.cumsum(hit_table, axis=0) - hit_table
    slot_rank = jnp.sum(earlier * hit_table, axis=1)
    dest_row = flat_ids * capacity + slot_rank
    fixed_gate = gate_fixed.astype(jnp.float32)
    gate_share = ROUTED_SCALE * fixed_gate / jnp.sum(fixed_gate, axis=1, keepdims=True)
    copies = in_one_piece((tokens, experts.astype(jnp.bfloat16)), "ep", 0, 1)
    all_tokens = copies[0]
    all_ids = copies[1].astype(jnp.int32)
    own_expert = lax.axis_index("ep") // shards
    named = jnp.any(all_ids == own_expert, axis=1).astype(jnp.int32).reshape(device_count, tok_rows)
    rank = jnp.cumsum(named, axis=1) - named
    base = jnp.arange(device_count, dtype=jnp.int32)[:, None] * capacity
    position = jnp.where(named > 0, base + rank, device_count * capacity).reshape(-1)
    incoming = (
        jnp.zeros((device_count * capacity, model_width), jnp.bfloat16)
        .at[position]
        .set(all_tokens, mode="drop")
    )
    results = expert_rows(incoming, w_gate, w_up, w_down).reshape(
        device_count, capacity, model_width
    )
    returned = several_exchanges(results, "ep", 2, 0, 0)
    loads = gathered_total(jnp.sum(hit_table, axis=0), "ep")
    summed = jnp.sum(
        returned.reshape(expert_count, shards, capacity, model_width), axis=1, dtype=jnp.float32
    )
    summed = summed.reshape(expert_count * capacity, model_width)
    picked = summed[dest_row].reshape(tok_rows, top_count, model_width)
    combined = jnp.sum(picked * gate_share[:, :, None], axis=1).astype(jnp.bfloat16)
    placer = (home_slot[None, :] == jnp.arange(tok_rows, dtype=jnp.int32)[:, None]).astype(
        jnp.bfloat16
    )
    placed = jnp.dot(placer, combined, preferred_element_type=jnp.float32).astype(jnp.bfloat16)
    average = tok_rows * device_count * top_count / expert_count
    bias_next = bias + 2.0 / math.sqrt(average) * (average - loads.astype(jnp.float32))
    return (placed, bias_next)


def solution(mesh):
    placed = (
        P(("groups", "ep"), None),
        P(("groups", "ep"), None),
        P(("groups", "ep"), None),
        P(("groups", "ep")),
        P(),
        P(None, "ep"),
        P(None, "ep"),
        P("ep", None),
    )
    return jax.shard_map(
        per_device,
        mesh=mesh,
        in_specs=placed,
        out_specs=(P(("groups", "ep"), None), P("groups")),
        check_vma=False,
    )
```

profile of v0, /device:TPU:513, one launch (start us, length us, event | category | flops | bytes accessed | tf_op | source)
XLA Modules:
  0.0 656.1 jit_solution(9724134064194463456)
XLA Ops:
  7.2 0.1 all-gather.3.cloned.1.call-start
  7.2 0.8 broadcast_multiply_fusion
  8.0 1.5 pad_maximum_fusion.1
  9.6 0.1 all-gather.3.cloned.1.call-update
  9.6 0.1 add.60
  9.7 0.1 add.61
  9.8 112.8 %all-gather.3.cloned.1.call-done = bf16[1024,7176]{1,0:T(8,128)(2,1)} async-done(((bf16[8,7176]{1,0:T(8,128)(2,1)}), bf16[1024,7176]{1,0:T(8,128)(2,1)}) %all-gather.3.cloned.1.call-update) | async-done | bytes 14696464 | tf_op jit(solution)/shard_map/all_gather | solution.py:17
  122.7 1.2 fusion.10
  123.8 0.1 reshape.104
  123.9 0.2 reduce_window_sum.24
  124.1 0.1 reduce_window_sum.25
  124.2 27.4 %scatter_custom_fusion = bf16[768,7168]{1,0:T(8,128)(2,1)} fusion(s32[1024]{0:T(1024)S(1)} %bitcast.29, bf16[1024,7176]{1,0:T(8,128)(2,1)} %all-gather.3.cloned.1.call-done, bf16[]{:T(256)} %constant.16.clone.1), kind=kCustom, calls=%fused_computation.3 | custom fusion | bytes 25690624 | tf_op jit(solution)/shard_map/scatter | solution.py:88
  151.6 6.9 %fusion.18 = f32[768,256]{1,0:T(8,128)S(1)} fusion(bf16[768,7168]{1,0:T(8,128)(2,1)} %scatter_custom_fusion, bf16[7168,256]{1,0:T(8,128)(2,1)} %param.13), kind=kOutput, calls=%fused_computation.43 | convolution fusion | flops 2818572288 | bytes 15466496 | tf_op jit(solution)/shard_map/dot_general | solution.py:52
  158.5 18.8 %convolution_convert_fusion = bf16[768,7168]{1,0:T(8,128)(2,1)} fusion(bf16[256,7168]{1,0:T(8,128)(2,1)} %param.15, bf16[768,7168]{1,0:T(8,128)(2,1)} %scatter_custom_fusion, bf16[7168,256]{1,0:T(8,128)(2,1)} %param.14, f32[768,256]{1,0:T(8,128)S(1)} %fusion.18), kind=kOutput, calls=%fused_computation.6 | convolution fusion | flops 5643829248 | bytes 30146560 | tf_op jit(solution)/shard_map/dot_general | solution.py:55
  177.3 15.9 %reshape_reshape.4 = bf16[128,1,6,7168]{3,2,0,1:T(8,128)(2,1)} reshape(bf16[768,7168]{1,0:T(8,128)(2,1)} %convolution_convert_fusion) | data formatting | bytes 22020096 | tf_op jit(solution)/shard_map/reshape;reshape | solution.py:22
  193.2 16.7 %slice_bitcast_fusion.1 = (bf16[128,1,3,7168]{3,2,1,0:T(4,128)(2,1)S(1)}, bf16[128,1,3,7168]{3,2,1,0:T(4,128)(2,1)}) fusion(bf16[128,1,6,7168]{3,2,0,1:T(8,128)(2,1)} %reshape_reshape.4), kind=kLoop, calls=%fused_computation.9 | loop fusion | bytes 22020096 | tf_op jit(solution)/shard_map/split | solution.py:40
  210.0 174.4 %all_to_all.10 = bf16[128,1,3,7168]{3,2,1,0:T(4,128)(2,1)} all-to-all(bf16[128,1,3,7168]{3,2,1,0:T(4,128)(2,1)S(1)} %get-tuple-element.4), channel_id=1, replica_groups=mesh['groups'=2,'ep'=128] {'ep'}, dimensions={0} | all-to-all | bytes 11010048 | tf_op jit(solution)/shard_map/all_to_all | solution.py:42
  384.4 0.0 copy-start
  384.4 0.0 copy-start.4
  384.4 0.0 copy-start.1
  384.4 0.0 copy-start.3
  384.4 26.4 %all-to-all-start.1 = ((bf16[128,1,3,7168]{3,2,1,0:T(4,128)(2,1)}), bf16[128,1,3,7168]{3,2,1,0:T(4,128)(2,1)}, u32[]{:S(2)}, u32[]{:S(2)}) async-start(bf16[128,1,3,7168]{3,2,1,0:T(4,128)(2,1)} %get-tuple-element.5), calls=%async_computation.1 | async-start | bytes 14680064 | tf_op jit(solution)/shard_map/all_to_all | solution.py:42
  410.8 0.0 copy-done
  410.8 0.1 eq.39
  410.9 0.1 fusion.13
  411.0 0.1 reduce_window_sum.26
  411.1 0.1 mul.60
  411.1 0.0 copy-done.4
  411.1 0.6 dynamic-slice
  412.4 0.2 fusion.14
  412.6 0.3 dynamic-update-slice
  412.8 211.7 %all-reduce = s32[2048]{0:T(1024)S(1)} all-reduce(s32[2048]{0:T(1024)S(1)} %dynamic-update-slice), channel_id=2, replica_groups=mesh['groups'=2,'ep'=128] {'ep'}, use_global_device_ids=true, to_apply=%add | all-reduce | flops 2048 | bytes 16384
  624.6 0.1 reshape.122
  624.7 0.0 copy-done.1
  624.7 0.1 convert_reduce_fusion.1
  624.8 0.0 copy-done.3
  624.8 0.5 multiply_add_fusion
  625.3 0.1 multiply_divide_fusion
  625.4 0.0 all-to-all-done.1
  625.4 10.4 %pad_maximum_fusion = bf16[128,1,6,7168]{3,2,1,0:T(8,128)(2,1)S(1)} fusion(bf16[128,1,3,7168]{3,2,1,0:T(4,128)(2,1)} %all-to-all-done.1, bf16[128,1,3,7168]{3,2,1,0:T(4,128)(2,1)} %all_to_all.10), kind=kLoop, calls=%fused_computation.5 | loop fusion | flops 22020096 | bytes 22020096 | tf_op jit(solution)/shard_map/concatenate | solution.py:43
  635.8 5.9 convert_reduce_fusion
  641.7 0.0 copy-start.2
  641.7 2.3 reshape.101
  644.0 2.3 gather_fusion
  646.3 2.1 fusion.3
  648.4 0.0 copy-done.2
  648.5 0.8 convolution_convert_fusion.1
  (7 shorter events, 0.1 us)
Async XLA Ops:
  7.2 115.5 %all-gather.3.cloned.1.call-start = ((), (), s32[]{:S(2)}) async-start(), calls=%async_computation.2 | async-start | bytes 15058944 | tf_op jit(solution)/shard_map/all_gather | solution.py:17
  384.4 26.4 %copy-start = (s32[8,8]{1,0:T(8,128)S(1)}, s32[8,8]{1,0:T(8,128)}, u32[]{:S(2)}) copy-start(s32[8,8]{1,0:T(8,128)} %param.9) | copy-start | bytes 772
  384.4 26.7 %copy-start.4 = (u32[256]{0:T(256)S(1)}, u32[256]{0:T(256)}, u32[]{:S(2)}) copy-start(u32[256]{0:T(256)} %constant.60) | copy-start | bytes 3076
  384.4 240.3 %copy-start.1 = (s32[8,8]{1,0:T(8,128)S(1)}, s32[8,8]{1,0:T(8,128)}, u32[]{:S(2)}) copy-start(s32[8,8]{1,0:T(8,128)} %param.10) | copy-start | bytes 772
  384.4 240.4 %copy-start.3 = (f32[16]{0:T(128)S(1)}, f32[16]{0:T(128)}, u32[]{:S(2)}) copy-start(f32[16]{0:T(128)} %param.12) | copy-start | bytes 196
  384.4 241.0 %all-to-all-start.1 = ((bf16[128,1,3,7168]{3,2,1,0:T(4,128)(2,1)}), bf16[128,1,3,7168]{3,2,1,0:T(4,128)(2,1)}, u32[]{:S(2)}, u32[]{:S(2)}) async-start(bf16[128,1,3,7168]{3,2,1,0:T(4,128)(2,1)} %get-tuple-element.5), calls=%async_computation.1 | async-start | bytes 14680064 | tf_op jit(solution)/shard_map/all_to_all | solution.py:42
  641.7 6.8 %copy-start.2 = (s32[8]{0:T(128)S(1)}, s32[8]{0:T(128)}, u32[]{:S(2)}) copy-start(s32[8]{0:T(128)} %param.11) | copy-start | bytes 100
Sparse Core Ops, SparseCore 0:
  10.7 111.9 all-gather.2
where the time goes:
time: 660 us; the launch traced here: 656 us
  blocking collectives  386 us (58%)
  waiting for transfers between devices  113 us (17%)
  local copies, waits for them, and re-layouts  66.1 us (10%)
  matrix products  26.5 us (4%)
  starting transfers between devices  26.4 us (4%)
  other arithmetic  23.2 us (4%)
  between operations  14.9 us (2%)
    unnamed x1, blocking collectives  212 us
    all_to_all x1, blocking collectives, several_exchanges(): lax.all_to_all(piece, axis, split_axis=0, concat_axis=0, tiled=True)  174 us
    all_gather x1, waiting for transfers between devices, in_one_piece(): lax.all_gather(both, axis, axis=dim, tiled=True)  113 us
    scatter x1, local copies, waits for them, and re-layouts, per_device(): incoming = jnp.zeros((device_count * capacity, model_width), jnp.bfloat16...  27.4 us
    all_to_all x1, starting transfers between devices, several_exchanges(): lax.all_to_all(piece, axis, split_axis=0, concat_axis=0, tiled=True)  26.4 us
    dot_general x1, matrix products, expert_rows(): jnp.dot(hidden, w_down, preferred_element_type=jnp.float32)  18.8 us
    split x1, local copies, waits for them, and re-layouts, several_exchanges(): jnp.split(tiles, cut_rows(tiles.shape[cut], pieces), axis=cut)  16.7 us
    another operation x1, local copies, waits for them, and re-layouts, in_blocks(): return jnp.moveaxis(array.reshape(*before, devices, -1, *after), dim, 0)  15.9 us
  transfers between devices with their start and end apart: 2, of which 1 were waited for; matrix products, arithmetic and copies ran while one was open for 0% of the time, Pallas kernels for 0%

commit v1 on v0

v1 whole, which is shorter than its diff:
```python
import math

import jax
import jax.numpy as jnp
from jax import lax
from jax.sharding import PartitionSpec as P

ROUTED_SCALE = 2.5


def per_device(tokens, experts, gate_fixed, home_slot, bias, w_gate, w_up, w_down):
    tok_rows, width = tokens.shape
    top_count = experts.shape[1]
    expert_count = bias.shape[0]
    device_count = lax.axis_size("ep")
    shards = device_count // expert_count
    meta = jnp.concatenate([experts, gate_fixed // 256, gate_fixed % 256], axis=1)
    rows = jnp.concatenate([tokens, meta.astype(jnp.bfloat16)], axis=1)
    placer = (home_slot[None, :] == jnp.arange(tok_rows, dtype=jnp.int32)[:, None]).astype(jnp.bfloat16)
    rows = jnp.dot(placer, rows, preferred_element_type=jnp.float32).astype(jnp.bfloat16)
    everyone = lax.all_gather(rows, "ep", axis=0, tiled=True)
    x = everyone[:, :width]
    meta = everyone[:, width:].astype(jnp.float32)
    ids, high, low = meta[:, :top_count], meta[:, top_count : 2 * top_count], meta[:, 2 * top_count :]
    fixed = high * 256.0 + low
    share = ROUTED_SCALE * fixed / jnp.sum(fixed, axis=1, keepdims=True)
    own = (lax.axis_index("ep") // shards).astype(jnp.float32)
    gate = jnp.sum(jnp.where(ids == own, share, 0.0), axis=1, keepdims=True)
    gate_part = jnp.dot(x, w_gate, preferred_element_type=jnp.float32)
    up_part = jnp.dot(x, w_up, preferred_element_type=jnp.float32)
    hidden = (jax.nn.silu(gate_part) * up_part * gate).astype(jnp.bfloat16)
    part = jnp.dot(hidden, w_down, preferred_element_type=jnp.float32).astype(jnp.bfloat16)
    out = lax.psum_scatter(part, "ep", scatter_dimension=0, tiled=True)
    hits = ids[:, :, None] == jnp.arange(expert_count, dtype=jnp.float32)[None, None, :]
    loads = jnp.sum(hits.astype(jnp.float32), axis=(0, 1))
    average = tok_rows * device_count * top_count / expert_count
    bias_next = bias + 2.0 / math.sqrt(average) * (average - loads)
    return (out, bias_next)


def solution(mesh):
    placed = (
        P(("groups", "ep"), None),
        P(("groups", "ep"), None),
        P(("groups", "ep"), None),
        P(("groups", "ep")),
        P(),
        P(None, "ep"),
        P(None, "ep"),
        P("ep", None),
    )
    return jax.shard_map(
        per_device,
        mesh=mesh,
        in_specs=placed,
        out_specs=(P(("groups", "ep"), None), P("groups")),
        check_vma=False,
    )
```

time: 660 us -> 376 us (0.57)
  blocking collectives: 386 us -> 0 us
  waiting for transfers between devices: 113 us -> 319 us
  local copies, waits for them, and re-layouts: 66.1 us -> 1.37 us
  starting transfers between devices: 26.4 us -> 0.13 us
  other arithmetic: 23.2 us -> 4.24 us
  matrix products: 26.5 us -> 33.4 us
    unnamed x1 -> x0, blocking collectives: 212 us -> none
    reduce_scatter x0 -> x1, waiting for transfers between devices: none -> 207 us  [per_device(): out = lax.psum_scatter(part, 'ep', scatter_dimension=0, tiled=True)]
    all_to_all x1 -> x0, blocking collectives: 174 us -> none  [several_exchanges(): lax.all_to_all(piece, axis, split_axis=0, concat_axis=0, tiled=True)]
    scatter x1 -> x0, local copies, waits for them, and re-layouts: 27.4 us -> none  [per_device(): incoming = jnp.zeros((device_count * capacity, model_width), jnp.bfloat16...]
    all_to_all x1 -> x0, starting transfers between devices: 26.4 us -> none  [several_exchanges(): lax.all_to_all(piece, axis, split_axis=0, concat_axis=0, tiled=True)]
    split x1 -> x0, local copies, waits for them, and re-layouts: 16.7 us -> none  [several_exchanges(): jnp.split(tiles, cut_rows(tiles.shape[cut], pieces), axis=cut)]
    another operation x2 -> x0, local copies, waits for them, and re-layouts: 16 us -> none  [the longest x1 15.9 us: in_blocks(): return jnp.moveaxis(array.reshape(*before, devices, -1, *after), dim, 0)]
    concatenate x2 -> x0, other arithmetic: 11.9 us -> none  [the longest x1 10.4 us: several_exchanges(): return in_order(jnp.concatenate(outs, axis=cut), concat_dim)]
  transfers between devices with their start and end apart: 2 -> 2, of which waited for: 1 -> 2; matrix products, arithmetic and copies ran while one was open for 0% -> 0% of each run, Pallas kernels for 0% -> 0%
where the time goes in v1:
time: 376 us; the launch traced here: 372 us
  waiting for transfers between devices  319 us (85%)
  matrix products  33.4 us (9%)
  between operations  14.1 us (4%)
  other arithmetic  4.24 us (1%)
    reduce_scatter x1, waiting for transfers between devices, per_device(): out = lax.psum_scatter(part, 'ep', scatter_dimension=0, tiled=True)  207 us
    all_gather x1, waiting for transfers between devices, per_device(): everyone = lax.all_gather(rows, 'ep', axis=0, tiled=True)  112 us
    dot_general x1, matrix products, per_device(): jnp.dot(hidden, w_down, preferred_element_type=jnp.float32)  23.7 us
    dot_general x1, matrix products, per_device(): gate_part = jnp.dot(x, w_gate, preferred_element_type=jnp.float32)  8.3 us
  transfers between devices with their start and end apart: 2, of which 2 were waited for; matrix products, arithmetic and copies ran while one was open for 0% of the time, Pallas kernels for 0%

profile of v1, /device:TPU:513, one launch (start us, length us, event | category | flops | bytes accessed | tf_op | source)
XLA Modules:
  0.0 372.4 jit_solution(18024475353310165763)
XLA Ops:
  7.2 0.1 all-gather.2.cloned.1.call-start
  7.2 0.7 convert.9
  7.9 0.7 fusion.24
  8.6 1.0 concatenate.6
  9.6 1.5 convolution_convert_fusion.1
  11.1 0.1 all-gather.2.cloned.1.call-update
  11.1 0.1 reduce-scatter.2.cloned.1.call-start
  11.2 112.0 %all-gather.2.cloned.1.call-done = bf16[1024,7192]{1,0:T(8,128)(2,1)} async-done(((bf16[8,7192]{1,0:T(8,128)(2,1)}), bf16[1024,7192]{1,0:T(8,128)(2,1)}) %all-gather.2.cloned.1.call-update) | async-done | bytes 14729232 | tf_op jit(solution)/shard_map/all_gather | solution.py:21
  123.2 1.0 slice_convert_fusion
  124.2 0.5 fusion.29
  124.7 0.6 select_reduce_fusion
  125.4 8.3 %fusion.2 = f32[1024,256]{1,0:T(8,128)S(1)} fusion(bf16[7168,256]{1,0:T(8,128)(2,1)} %param.13, bf16[1024,7192]{1,0:T(8,128)(2,1)} %all-gather.2.cloned.1.call-done), kind=kOutput, calls=%fused_computation.3 | convolution fusion | flops 3758096384 | bytes 19398656 | tf_op jit(solution)/shard_map/dot_general | solution.py:29
  133.7 23.7 %convolution_convert_fusion = bf16[1024,7168]{1,0:T(8,128)(2,1)} fusion(bf16[256,7168]{1,0:T(8,128)(2,1)} %param.15, bf16[7168,256]{1,0:T(8,128)(2,1)} %param.14, bf16[1024,7192]{1,0:T(8,128)(2,1)} %all-gather.2.cloned.1.call-done, f32[1024,256]{1,0:T(8,128)S(1)} %fusion.2, f32[1024]{0:T(1024)S(1)} %select_reduce_fusion), kind=kOutput, calls=%fused_computation | convolution fusion | flops 7525367808 | bytes 37752832 | tf_op jit(solution)/shard_map/dot_general | solution.py:32
  157.4 0.0 copy-start
  157.4 0.1 reduce-scatter.2.cloned.1.call-update
  157.4 0.2 copy.10
  157.6 0.2 convert_reduce_fusion
  157.8 0.2 copy-done
  158.0 0.5 multiply_add_fusion
  158.5 207.0 %reduce-scatter.2.cloned.1.call-done = bf16[8,7168]{1,0:T(8,128)(2,1)} async-done(((bf16[1024,7168]{1,0:T(8,128)(2,1)}), bf16[8,7168]{1,0:T(8,128)(2,1)}) %reduce-scatter.2.cloned.1.call-update) | async-done | bytes 114704 | tf_op jit(solution)/shard_map/reduce_scatter | solution.py:33
Async XLA Ops:
  7.2 116.1 %all-gather.2.cloned.1.call-start = ((), (), s32[]{:S(2)}) async-start(), calls=%async_computation.1 | async-start | bytes 15058944 | tf_op jit(solution)/shard_map/all_gather | solution.py:21
  11.1 354.4 %reduce-scatter.2.cloned.1.call-start = ((), (), s32[]{:S(2)}) async-start(), calls=%async_computation.2 | async-start | bytes 14794752 | tf_op jit(solution)/shard_map/reduce_scatter | solution.py:33
  157.4 0.7 copy-start
Sparse Core Ops, SparseCore 0:
  11.3 111.9 all-gather.1
  157.5 207.9 reduce-scatter.1

commit v2 on v1

v2 whole, which is shorter than its diff:
```python
import functools
import math

import jax
import jax.numpy as jnp
from jax import lax
from jax.experimental import pallas as pl
from jax.experimental.pallas import tpu as pltpu
from jax.sharding import PartitionSpec as P

ROUTED_SCALE = 2.5
F32 = jnp.float32
BF16 = jnp.bfloat16


def when(cond):
    return pl.when(cond)


def kernel(
    dims, home, tok, exp_ref, gate_ref, bias_ref, wg, wu, wd,
    out, bias_out,
    xs, xr, x_own, x_par, wgu, wdn, acc, hid, pst, prx, ring, z_out, z_in, fin, f_out, f_in,
    w_sem, x_sem, s1, r1, s2, r2, sd, rd, sp, rp, sr, rr, sz, rz, sf,
):
    side, experts, shards, average = dims
    R, H = side, side // 2
    top = exp_ref.shape[1]
    half = tok.shape[1] // 2
    wide = half + 128
    cut = (half // 2) // 128 * 128
    ff = wg.shape[1]
    me = lax.axis_index("ep")
    core = me % 2
    x = (me // 2) % side
    y = me // (2 * side)
    a = y + core * (x - y)
    b = x + core * (y - x)

    def device(aa, bb):
        yy = aa + core * (bb - aa)
        xx = bb + core * (aa - bb)
        return {"ep": (yy * side + xx) * 2 + core}

    a_next, a_prev = device((a + 1) % R, b), device((a + R - 1) % R, b)
    b_next, b_prev = device(a, (b + 1) % R), device(a, (b + R - 1) % R)
    partner = {"ep": me + 1 - 2 * core}
    b_to = (b_next, b_prev)

    def remote(src, dst, send, recv, to):
        return pltpu.make_async_remote_copy(
            src_ref=src, dst_ref=dst, send_sem=send, recv_sem=recv,
            device_id=to, device_id_type=pl.DeviceIdType.MESH,
        )

    weights = []
    for h in range(2):
        rows = pl.ds(h * half, half)
        weights.append(pltpu.make_async_copy(wg.at[rows, :], wgu.at[h, :, pl.ds(0, ff)], w_sem.at[3 * h]))
        weights.append(pltpu.make_async_copy(wu.at[rows, :], wgu.at[h, :, pl.ds(ff, ff)], w_sem.at[3 * h + 1]))
        weights.append(pltpu.make_async_copy(wd.at[:, rows], wdn.at[h], w_sem.at[3 * h + 2]))
    for w in weights:
        w.start()

    barrier = pltpu.get_barrier_semaphore()
    for to in (partner, a_next, a_prev, b_next, b_prev):
        pl.semaphore_signal(barrier, inc=1, device_id=to, device_id_type=pl.DeviceIdType.MESH)

    fixed = gate_ref[...].astype(F32)
    share = ROUTED_SCALE * fixed / jnp.sum(fixed, axis=1, keepdims=True)
    ids = exp_ref[...]
    lane = lax.broadcasted_iota(jnp.int32, (tok.shape[0], 128), 1)
    expert_of = lane % experts
    hit = jnp.zeros(lane.shape, F32)
    val = jnp.zeros(lane.shape, F32)
    for k in range(top):
        same = expert_of == ids[:, k : k + 1]
        hit = hit + jnp.where(same, 1.0, 0.0)
        val = val + jnp.where(same, share[:, k : k + 1], 0.0)
    high = val.astype(BF16).astype(F32)
    rest = val - high
    mid = rest.astype(BF16).astype(F32)
    low = rest - mid
    part = lane // experts
    meta = jnp.where(part == 0, hit, 0.0)
    meta = jnp.where(part == 1, high, meta)
    meta = jnp.where(part == 2, mid, meta)
    meta = jnp.where(part == 3, low, meta)
    first = core == 0
    lo_half = tok[:, pl.ds(0, half)].astype(F32)
    hi_half = tok[:, pl.ds(half, half)].astype(F32)
    mine = jnp.where(first, lo_half, hi_half)
    xs[:, pl.ds(0, half)] = jnp.where(first, hi_half, lo_half).astype(BF16)
    xs[:, pl.ds(half, 128)] = meta.astype(BF16)

    pl.semaphore_wait(barrier, 5)
    swap = remote(xs, xr, x_sem.at[0], x_sem.at[1], partner)
    swap.start()
    swap.wait_recv()
    got = xr[...].astype(F32)
    x_own[0, 0, :, pl.ds(0, half)] = jnp.where(
        first,
        jnp.concatenate([mine, got[:, :half]], axis=0),
        jnp.concatenate([got[:, :half], mine], axis=0),
    ).astype(BF16)
    x_own[0, 0, :, pl.ds(half, 128)] = jnp.where(
        first,
        jnp.concatenate([meta, got[:, half:]], axis=0),
        jnp.concatenate([got[:, half:], meta], axis=0),
    ).astype(BF16)

    def down(g):
        src = jnp.maximum(2 * g - 1, 0) if not isinstance(g, int) else max(2 * g - 1, 0)
        return remote(x_own.at[0, src], x_own.at[0, 2 * g + 1], s1.at[1, g], r1.at[1, g], a_prev)

    def up(g):
        return remote(x_own.at[0, 2 * g], x_own.at[0, 2 * g + 2], s1.at[0, g], r1.at[0, g], a_next)

    down(0).start()
    up(0).start()

    def clear(j, c):
        for d in range(2):
            ring[d, H, j] = jnp.zeros((16, half), BF16)
        ring[0, H - 1, j, :, pl.ds(cut, half - cut)] = jnp.zeros((16, half - cut), BF16)
        ring[1, H - 1, j, :, pl.ds(0, cut)] = jnp.zeros((16, cut), BF16)
        acc[j] = jnp.zeros(acc.shape[1:], F32)
        return c

    lax.fori_loop(0, R, clear, 0)
    for d in range(2):
        z_in[d, H] = jnp.zeros((16, half), BF16)

    whole = pl.ds(0, wide)
    lows, highs = pl.ds(0, cut), pl.ds(cut, wide - cut)

    def ring_x(d, s, g, cols):
        n = s if d == 0 else (R - s) % R
        to = s + 1 if d == 0 else R - s - 1
        return remote(
            x_own.at[n, pl.ds(2 * g, 2), :, cols], x_own.at[to, pl.ds(2 * g, 2), :, cols],
            s2.at[d, s, g], r2.at[d, s, g], b_to[d],
        )

    def across(n, g):
        return remote(
            x_own.at[n, pl.ds(2 * g, 2)], x_par.at[n, pl.ds(2 * g, 2)], sd.at[n, g], rd.at[n, g], partner
        )

    def gather_step(k, g):
        s = k - g

        @when(s == 0)
        def _():
            down(g).wait_recv()

            @when(g < H - 1)
            def _():
                down(g + 1).start()
                up(g).wait_recv()

            @when(g < H - 2)
            def _():
                up(g + 1).start()

        @when((s >= 1) & (s < H))
        def _():
            for d in range(2):
                ring_x(d, s - 1, g, whole).wait_recv()

        @when(s == H)
        def _():
            ring_x(0, H - 1, g, lows).wait_recv()
            ring_x(1, H - 1, g, highs).wait_recv()

        @when((s >= 0) & (s < H - 1))
        def _():
            for d in range(2):
                ring_x(d, s, g, whole).start()

        @when(s == H - 1)
        def _():
            ring_x(0, H - 1, g, lows).start()
            ring_x(1, H - 1, g, highs).start()

        @when((s >= 0) & (s <= H))
        def _():
            across(s, g).start()

        @when((s >= 1) & (s < H))
        def _():
            across(R - s, g).start()

    def own_block(n):
        rows = x_own[n, :, :, pl.ds(0, half)].reshape(R * 16, half)
        prod = jnp.dot(rows, wgu[core], preferred_element_type=F32)
        acc[n] += prod.reshape(R, 16, 2 * ff)

    def slot_of(n):
        return jnp.where(n < H, 2 * n, 2 * R - 1 - 2 * n)

    def par_block(n):
        for g in range(H):
            across(n, g).wait_recv()
        rows = x_par[n, :, :, pl.ds(0, half)].reshape(R * 16, half)
        prod = jnp.dot(rows, wgu[1 - core], preferred_element_type=F32)
        j = slot_of(n)
        for t in range(R):
            m = t // 2 if t % 2 == 0 else R - 1 - t // 2
            acc[m, j] += prod[16 * t : 16 * t + 16]

    def gather_stage(k, c):
        lax.fori_loop(0, H, lambda g, cc: (gather_step(k, g), cc)[1], 0)

        @when(k == H - 1)
        def _():
            for w in weights:
                w.wait()

        @when(k >= H - 1)
        def _():
            s = k - (H - 1)
            count = jnp.where((s >= 1) & (s < H), 2, 1)

            def own(i, cc):
                own_block(s + i * (R - 2 * s))
                return cc

            def par(i, cc):
                par_block(s + i * (R - 2 * s))
                return cc

            lax.fori_loop(0, count, own, 0)
            lax.fori_loop(0, count, par, 0)

        return c

    lax.fori_loop(0, 2 * H, gather_stage, 0)

    my_expert = me // shards
    lane = lax.broadcasted_iota(jnp.int32, (R * 16, 128), 1)
    gated = (lane % experts == my_expert) & (lane >= experts) & (lane < 4 * experts)

    def activate(n, total):
        m = x_own[n, :, :, pl.ds(half, 128)].reshape(R * 16, 128).astype(F32)
        gate = jnp.sum(jnp.where(gated, m, 0.0), axis=1, keepdims=True)
        both = acc[n].reshape(R * 16, 2 * ff)
        v = both[:, :ff]
        h = v / (1.0 + jnp.exp(-v)) * both[:, ff:] * gate
        hid[n] = h.astype(BF16).reshape(R, 16, ff)
        return total + jnp.sum(m, axis=0, keepdims=True)

    loads = lax.fori_loop(0, R, activate, jnp.zeros((1, 128), F32))
    bias_out[...] = bias_ref[...] + 2.0 / math.sqrt(average) * (average - loads[:, :experts])

    C = 512 if half % 512 == 0 else 128

    def to_partner(g, s):
        return remote(pst.at[g, s], prx.at[g, s], sp.at[g, s], rp.at[g, s], partner)

    def partner_chunk(g, s):
        j1, j2 = slot_of((R - s) % R), slot_of(s)
        lhs = jnp.concatenate(
            [hid[g, j1], hid[R - 1 - g, j1], hid[g, j2], hid[R - 1 - g, j2]], axis=0
        )

        def cols(t, cc):
            at = pl.ds(pl.multiple_of(t * C, 128), C)
            p = jnp.dot(lhs, wdn[1 - core, :, at], preferred_element_type=F32)
            pst[g, s, :, :, :, at] = p.astype(BF16).reshape(2, 2, 16, C)
            return cc

        lax.fori_loop(0, half // C, cols, 0)
        to_partner(g, s).start()

    whole_z = pl.ds(0, half)
    lows_z, highs_z = pl.ds(0, cut), pl.ds(cut, half - cut)

    def ring_r(d, s, g, cols):
        return remote(
            ring.at[d, s, pl.ds(2 * g, 2), :, cols], ring.at[d, s - 1, pl.ds(2 * g, 2), :, cols],
            sr.at[d, s - 1, g], rr.at[d, s - 1, g], b_to[d],
        )

    def z_up(g):
        return remote(z_out.at[0, g], z_in.at[0, g], sz.at[0, g], rz.at[0, g], a_next)

    def z_down(g):
        return remote(z_out.at[1, g], z_in.at[1, g], sz.at[1, g], rz.at[1, g], a_prev)

    def own_chunk(g, s):
        to_partner(g, s).wait_recv()

        @when(s < H - 1)
        def _():
            for d in range(2):
                ring_r(d, s + 1, g, whole_z).wait_recv()

        @when(s == H - 1)
        def _():
            ring_r(0, H, g, lows_z).wait_recv()
            ring_r(1, H, g, highs_z).wait_recv()

        pair = pl.ds(2 * g, 2)

        @when(s >= 1)
        def _():
            lhs = jnp.concatenate(
                [hid[(R - s) % R, pair].reshape(32, ff), hid[s, pair].reshape(32, ff)], axis=0
            )

            def cols(t, cc):
                at = pl.ds(pl.multiple_of(t * C, 128), C)
                p = jnp.dot(lhs, wdn[core, :, at], preferred_element_type=F32).reshape(2, 2, 16, C)
                p = p + prx[g, s, :, :, :, at].astype(F32)
                for d in range(2):
                    ring[d, s, pair, :, at] = (p[d] + ring[d, s, pair, :, at].astype(F32)).astype(BF16)
                return cc

            lax.fori_loop(0, half // C, cols, 0)

            @when(s < H)
            def _():
                for d in range(2):
                    ring_r(d, s, g, whole_z).start()

            @when(s == H)
            def _():
                ring_r(0, H, g, lows_z).start()
                ring_r(1, H, g, highs_z).start()

        @when(s == 0)
        def _():
            @when(g < H - 1)
            def _():
                z_up(g + 1).wait_recv()
                z_down(g + 1).wait_recv()

            lhs = hid[0, pair].reshape(32, ff)

            def cols(t, cc):
                at = pl.ds(pl.multiple_of(t * C, 128), C)
                p = jnp.dot(lhs, wdn[core, :, at], preferred_element_type=F32).reshape(2, 16, C)
                p = p + prx[g, 0, 0, :, :, at].astype(F32)
                p = p + ring[0, 0, pair, :, at].astype(F32) + ring[1, 0, pair, :, at].astype(F32)
                near = p[0] + z_in[1, g + 1, :, at].astype(F32)
                far = p[1] + z_in[0, g + 1, :, at].astype(F32)
                fin[:, at] = near
                z_out[1, g, :, at] = near.astype(BF16)
                z_out[0, g, :, at] = far.astype(BF16)
                return cc

            lax.fori_loop(0, half // C, cols, 0)
            z_up(g).start()

            @when(g >= 1)
            def _():
                z_down(g).start()

    def sum_stage(k, c):
        def own(i, cc):
            s = H - (k - 1) + i

            @when((s >= 0) & (s <= H) & (k >= 1))
            def _():
                own_chunk(H - 1 - i, s)

            return cc

        def other(i, cc):
            s = H - k + i

            @when((s >= 0) & (s <= H))
            def _():
                partner_chunk(H - 1 - i, s)

            return cc

        lax.fori_loop(0, H, own, 0)
        lax.fori_loop(0, H, other, 0)
        return c

    lax.fori_loop(0, 2 * H + 1, sum_stage, 0)
    z_up(0).wait_recv()

    total = fin[...] + z_in[0, 0].astype(F32)
    f_out[...] = jnp.where(first, total[8:], total[:8])
    kept = jnp.where(first, total[:8], total[8:])
    last = remote(f_out, f_in, sf.at[0], sf.at[1], partner)
    last.start()
    row = lax.broadcasted_iota(jnp.int32, (8, half), 0)

    def place(v):
        v = v.astype(BF16).astype(F32)
        placed = jnp.zeros((8, half), F32)
        for t in range(8):
            placed = jnp.where(row == home[t], jnp.broadcast_to(v[t : t + 1], (8, half)), placed)
        return placed

    kept = place(kept)

    swap.wait_send()

    def drain_g(g, c):
        down(g).wait_send()

        @when(g < H - 1)
        def _():
            up(g).wait_send()

        def per_s(s, cc):
            @when(s < H - 1)
            def _():
                for d in range(2):
                    ring_x(d, s, g, whole).wait_send()

            @when(s == H - 1)
            def _():
                ring_x(0, H - 1, g, lows).wait_send()
                ring_x(1, H - 1, g, highs).wait_send()
                ring_r(0, H, g, lows_z).wait_send()
                ring_r(1, H, g, highs_z).wait_send()

            @when(s < H - 1)
            def _():
                for d in range(2):
                    ring_r(d, s + 1, g, whole_z).wait_send()

            return cc

        lax.fori_loop(0, H, per_s, 0)

        def per_n(n, cc):
            across(n, g).wait_send()
            return cc

        lax.fori_loop(0, R, per_n, 0)

        def per_p(s, cc):
            to_partner(g, s).wait_send()
            return cc

        lax.fori_loop(0, H + 1, per_p, 0)
        z_up(g).wait_send()

        @when(g >= 1)
        def _():
            z_down(g).wait_send()

        return c

    lax.fori_loop(0, H, drain_g, 0)

    last.wait()
    other = place(f_in[...])
    out[:, pl.ds(0, half)] = jnp.where(first, kept, other).astype(BF16)
    out[:, pl.ds(half, half)] = jnp.where(first, other, kept).astype(BF16)


def per_device(tokens, experts, gate_fixed, home_slot, bias, w_gate, w_up, w_down):
    tok_rows, width = tokens.shape
    count = bias.shape[0]
    devices = lax.axis_size("ep")
    shards = devices // count
    side = math.isqrt(devices // 2)
    R, H = side, side // 2
    half = width // 2
    ff = w_gate.shape[1]
    average = tok_rows * devices * experts.shape[1] / count
    vmem = pl.BlockSpec(memory_space=pltpu.VMEM)
    smem = pl.BlockSpec(memory_space=pltpu.SMEM)
    anywhere = pl.BlockSpec(memory_space=pl.ANY)
    dma = pltpu.SemaphoreType.DMA
    out, bias_next = pl.pallas_call(
        functools.partial(kernel, (side, count, shards, average)),
        out_shape=(
            jax.ShapeDtypeStruct((tok_rows, width), BF16),
            jax.ShapeDtypeStruct((1, count), F32),
        ),
        in_specs=[smem, vmem, vmem, vmem, vmem, anywhere, anywhere, anywhere],
        out_specs=(vmem, vmem),
        scratch_shapes=[
            pltpu.VMEM((tok_rows, half + 128), BF16),
            pltpu.VMEM((tok_rows, half + 128), BF16),
            pltpu.VMEM((R, R, 16, half + 128), BF16),
            pltpu.VMEM((R, R, 16, half + 128), BF16),
            pltpu.VMEM((2, half, 2 * ff), BF16),
            pltpu.VMEM((2, ff, half), BF16),
            pltpu.VMEM((R, R, 16, 2 * ff), F32),
            pltpu.VMEM((R, R, 16, ff), BF16),
            pltpu.VMEM((H, H + 1, 2, 2, 16, half), BF16),
            pltpu.VMEM((H, H + 1, 2, 2, 16, half), BF16),
            pltpu.VMEM((2, H + 1, R, 16, half), BF16),
            pltpu.VMEM((2, H, 16, half), BF16),
            pltpu.VMEM((2, H + 1, 16, half), BF16),
            pltpu.VMEM((16, half), F32),
            pltpu.VMEM((tok_rows, half), F32),
            pltpu.VMEM((tok_rows, half), F32),
            dma((6,)),
            dma((2,)),
            dma((2, H)),
            dma((2, H)),
            dma((2, H, H)),
            dma((2, H, H)),
            dma((R, H)),
            dma((R, H)),
            dma((H, H + 1)),
            dma((H, H + 1)),
            dma((2, H, H)),
            dma((2, H, H)),
            dma((2, H)),
            dma((2, H)),
            dma((2,)),
        ],
        compiler_params=pltpu.CompilerParams(
            collective_id=0, has_side_effects=True, vmem_limit_bytes=67_000_000
        ),
        name="routed_experts",
    )(home_slot, tokens, experts, gate_fixed, bias.reshape(1, count), w_gate, w_up, w_down)
    return (out, bias_next.reshape(count))


def solution(mesh):
    placed = (
        P(("groups", "ep"), None),
        P(("groups", "ep"), None),
        P(("groups", "ep"), None),
        P(("groups", "ep")),
        P(),
        P(None, "ep"),
        P(None, "ep"),
        P("ep", None),
    )
    return jax.shard_map(
        per_device,
        mesh=mesh,
        in_specs=placed,
        out_specs=(P(("groups", "ep"), None), P("groups")),
        check_vma=False,
    )
```

time: 376 us -> 155 us (0.41)
  waiting for transfers between devices: 319 us -> 0 us
  Pallas kernels: 0 us -> 152 us
  matrix products: 33.4 us -> 0 us
  between operations: 14.1 us -> 0.64 us
  other arithmetic: 4.24 us -> 0 us
    reduce_scatter x1 -> x0, waiting for transfers between devices: 207 us -> none  [per_device(): out = lax.psum_scatter(part, 'ep', scatter_dimension=0, tiled=True)]
    pallas_call x0 -> x1, Pallas kernels: none -> 152 us  [per_device(): pl.pallas_call(functools.partial(kernel, (side, count, shards, average)),...]
    all_gather x1 -> x0, waiting for transfers between devices: 112 us -> none  [per_device(): everyone = lax.all_gather(rows, 'ep', axis=0, tiled=True)]
    dot_general x3 -> x0, matrix products: 33.4 us -> none  [the longest x1 23.7 us: per_device(): jnp.dot(hidden, w_down, preferred_element_type=jnp.float32)]
  transfers between devices with their start and end apart: 2 -> 0, of which waited for: 2 -> 0; matrix products, arithmetic and copies ran while one was open for 0% -> 0% of each run, Pallas kernels for 0% -> 0%
where the time goes in v2:
time: 155 us
  Pallas kernels  152 us (98%)
  local copies, waits for them, and re-layouts  2.66 us (2%)
    pallas_call x1, Pallas kernels, per_device(): pl.pallas_call(functools.partial(kernel, (side, count, shards, average)),...  152 us

profile of v2, /device:TPU:513, one launch (start us, length us, event | category | flops | bytes accessed | tf_op | source)
XLA Modules:
  0.0 155.0 jit_solution(17170938976336337649)
XLA Ops:
  0.6 151.7 %routed_experts.1 = (bf16[8,7168]{1,0:T(8,128)(2,1)}, f32[1,16]{1,0:T(1,128)}) custom-call(s32[8]{0:T(128)} %home.1, bf16[8,7168]{1,0:T(8,128)(2,1)} %tok.1, s32[8,8]{1,0:T(8,128)} %exp_ref.1, s32[8,8]{1,0:T(8,128)} %gate_ref.1, f32[1,16]{1,0:T(1,128)} %bitcast.2, bf16[7168,256]{1,0:T(8,128)(2,1)} %wg.1, bf16[7168,256]{1,0:T(8,128)(2,1)} %wu.1, ...), custom_call_target="tpu_custom_call" | custom-call | tf_op jit(solution)/shard_map/routed_experts/pallas_call | solution.py:474
  152.4 1.6 %copy.12 = bf16[8,7168]{1,0:T(8,128)(2,1)} copy(bf16[8,7168]{1,0:T(8,128)(2,1)} %get-tuple-element.8) | data formatting | bytes 229376
  153.9 1.1 copy.13

commit v3 on v2

--- a/solution.py
+++ b/solution.py
@@ -20,7 +20,7 @@
 def kernel(
     dims, home, tok, exp_ref, gate_ref, bias_ref, wg, wu, wd,
     out, bias_out,
-    xs, xr, x_own, x_par, wgu, wdn, acc, hid, pst, prx, ring, z_out, z_in, fin, f_out, f_in,
+    xs, xr, x_own, x_par, wgu, wdn, acc_own, acc_par, hid, pst, prx, ring, z_out, z_in, fin, f_out, f_in, loads,
     w_sem, x_sem, s1, r1, s2, r2, sd, rd, sp, rp, sr, rr, sz, rz, sf,
 ):
     side, experts, shards, average = dims
@@ -63,7 +63,7 @@
         w.start()
 
     barrier = pltpu.get_barrier_semaphore()
-    for to in (partner, a_next, a_prev, b_next, b_prev):
+    for to in [partner, b_next, b_prev] + [device((a + i) % R, b) for i in range(1, R)]:
         pl.semaphore_signal(barrier, inc=1, device_id=to, device_id_type=pl.DeviceIdType.MESH)
 
     fixed = gate_ref[...].astype(F32)
@@ -93,7 +93,7 @@
     xs[:, pl.ds(0, half)] = jnp.where(first, hi_half, lo_half).astype(BF16)
     xs[:, pl.ds(half, 128)] = meta.astype(BF16)
 
-    pl.semaphore_wait(barrier, 5)
+    pl.semaphore_wait(barrier, R + 2)
     swap = remote(xs, xr, x_sem.at[0], x_sem.at[1], partner)
     swap.start()
     swap.wait_recv()
@@ -120,16 +120,11 @@
     up(0).start()
 
     def clear(j, c):
-        for d in range(2):
-            ring[d, H, j] = jnp.zeros((16, half), BF16)
         ring[0, H - 1, j, :, pl.ds(cut, half - cut)] = jnp.zeros((16, half - cut), BF16)
         ring[1, H - 1, j, :, pl.ds(0, cut)] = jnp.zeros((16, cut), BF16)
-        acc[j] = jnp.zeros(acc.shape[1:], F32)
         return c
 
     lax.fori_loop(0, R, clear, 0)
-    for d in range(2):
-        z_in[d, H] = jnp.zeros((16, half), BF16)
 
     whole = pl.ds(0, wide)
     lows, highs = pl.ds(0, cut), pl.ds(cut, wide - cut)
@@ -191,67 +186,69 @@
         def _():
             across(R - s, g).start()
 
-    def own_block(n):
-        rows = x_own[n, :, :, pl.ds(0, half)].reshape(R * 16, half)
-        prod = jnp.dot(rows, wgu[core], preferred_element_type=F32)
-        acc[n] += prod.reshape(R, 16, 2 * ff)
-
     def slot_of(n):
         return jnp.where(n < H, 2 * n, 2 * R - 1 - 2 * n)
 
-    def par_block(n):
-        for g in range(H):
-            across(n, g).wait_recv()
-        rows = x_par[n, :, :, pl.ds(0, half)].reshape(R * 16, half)
-        prod = jnp.dot(rows, wgu[1 - core], preferred_element_type=F32)
+    def pair(g):
+        return pl.ds(2 * g, 2)
+
+    def gate_up(x_ref, acc_ref, w, chunks):
+        at = [(n, pair(g)) for g, s in chunks for n in (s, (R - s) % R)]
+        rows = jnp.concatenate(
+            [x_ref[n, p, :, pl.ds(0, half)].reshape(32, half) for n, p in at], axis=0
+        )
+        prod = jnp.dot(rows, wgu[w], preferred_element_type=F32)
+        for i, (n, p) in enumerate(at):
+            acc_ref[n, p] = prod[32 * i : 32 * i + 32].reshape(2, 16, 2 * ff)
+
+    def arrivals(k, body):
+        def unit(u, c):
+            s0 = k - 2 * u
+            v0 = (s0 >= 0) & (s0 <= H)
+            v1 = (s0 >= 1) & (s0 <= H + 1)
+
+            @when(v0 | v1)
+            def _():
+                g0 = 2 * u + jnp.where(v0, 0, 1)
+                g1 = 2 * u + jnp.where(v1, 1, 0)
+                body(v0, v1, [(g0, k - g0), (g1, k - g1)])
+
+            return c
+
+        lax.fori_loop(0, H // 2, unit, 0)
+
+    def own_arrivals(v0, v1, chunks):
+        gate_up(x_own, acc_own, core, chunks)
+
+    def par_arrivals(v0, v1, chunks):
+        for v, (g, s) in zip((v0, v1), chunks):
+            @when(v)
+            def _(g=g, s=s):
+                across(s, g).wait_recv()
+
+                @when((s >= 1) & (s < H))
+                def _():
+                    across(R - s, g).wait_recv()
+
+        gate_up(x_par, acc_par, 1 - core, chunks)
+
+    my_expert = me // shards
+    lane = lax.broadcasted_iota(jnp.int32, (32, 128), 1)
+    gated = (lane % experts == my_expert) & (lane >= experts) & (lane < 4 * experts)
+
+    def activate(n, g):
+        m = x_own[n, pair(g), :, pl.ds(half, 128)].reshape(32, 128).astype(F32)
+        gate = jnp.sum(jnp.where(gated, m, 0.0), axis=1, keepdims=True)
         j = slot_of(n)
-        for t in range(R):
-            m = t // 2 if t % 2 == 0 else R - 1 - t // 2
-            acc[m, j] += prod[16 * t : 16 * t + 16]
-
-    def gather_stage(k, c):
-        lax.fori_loop(0, H, lambda g, cc: (gather_step(k, g), cc)[1], 0)
-
-        @when(k == H - 1)
-        def _():
-            for w in weights:
-                w.wait()
-
-        @when(k >= H - 1)
-        def _():
-            s = k - (H - 1)
-            count = jnp.where((s >= 1) & (s < H), 2, 1)
-
-            def own(i, cc):
-                own_block(s + i * (R - 2 * s))
-                return cc
-
-            def par(i, cc):
-                par_block(s + i * (R - 2 * s))
-                return cc
-
-            lax.fori_loop(0, count, own, 0)
-            lax.fori_loop(0, count, par, 0)
-
-        return c
-
-    lax.fori_loop(0, 2 * H, gather_stage, 0)
-
-    my_expert = me // shards
-    lane = lax.broadcasted_iota(jnp.int32, (R * 16, 128), 1)
-    gated = (lane % experts == my_expert) & (lane >= experts) & (lane < 4 * experts)
-
-    def activate(n, total):
-        m = x_own[n, :, :, pl.ds(half, 128)].reshape(R * 16, 128).astype(F32)
-        gate = jnp.sum(jnp.where(gated, m, 0.0), axis=1, keepdims=True)
-        both = acc[n].reshape(R * 16, 2 * ff)
+        both = acc_own[n, pair(g)].reshape(32, 2 * ff) + jnp.concatenate(
+            [acc_par[g, j], acc_par[R - 1 - g, j]], axis=0
+        )
         v = both[:, :ff]
         h = v / (1.0 + jnp.exp(-v)) * both[:, ff:] * gate
-        hid[n] = h.astype(BF16).reshape(R, 16, ff)
-        return total + jnp.sum(m, axis=0, keepdims=True)
-
-    loads = lax.fori_loop(0, R, activate, jnp.zeros((1, 128), F32))
-    bias_out[...] = bias_ref[...] + 2.0 / math.sqrt(average) * (average - loads[:, :experts])
+        hid[n, pair(g)] = h.astype(BF16).reshape(2, 16, ff)
+        loads[...] += jnp.sum(m, axis=0, keepdims=True)
+
+    loads[...] = jnp.zeros((1, 128), F32)
 
     C = 512 if half % 512 == 0 else 128
 
@@ -265,125 +262,147 @@
         )
 
         def cols(t, cc):
-            at = pl.ds(pl.multiple_of(t * C, 128), C)
+            at = pl.ds(t * C, C)
             p = jnp.dot(lhs, wdn[1 - core, :, at], preferred_element_type=F32)
             pst[g, s, :, :, :, at] = p.astype(BF16).reshape(2, 2, 16, C)
             return cc
 
-        lax.fori_loop(0, half // C, cols, 0)
+        for t in range(half // C):
+            cols(t, 0)
         to_partner(g, s).start()
+
+    def own_chunk(g, s):
+        lhs = jnp.concatenate(
+            [hid[(R - s) % R, pair(g)].reshape(32, ff), hid[s, pair(g)].reshape(32, ff)], axis=0
+        )
+        to_partner(g, s).wait_recv()
+
+        def cols(t, cc):
+            at = pl.ds(t * C, C)
+            p = jnp.dot(lhs, wdn[core, :, at], preferred_element_type=F32).reshape(2, 2, 16, C)
+            prx[g, s, :, :, :, at] = (p + prx[g, s, :, :, :, at].astype(F32)).astype(BF16)
+            return cc
+
+        for t in range(half // C):
+            cols(t, 0)
 
     whole_z = pl.ds(0, half)
     lows_z, highs_z = pl.ds(0, cut), pl.ds(cut, half - cut)
 
-    def ring_r(d, s, g, cols):
+    def ring_first(d, g):
+        cols = highs_z if d else lows_z
         return remote(
-            ring.at[d, s, pl.ds(2 * g, 2), :, cols], ring.at[d, s - 1, pl.ds(2 * g, 2), :, cols],
+            prx.at[g, H, d, :, :, cols], ring.at[d, H - 1, pair(g), :, cols],
+            sr.at[d, H - 1, g], rr.at[d, H - 1, g], b_to[d],
+        )
+
+    def ring_r(d, s, g):
+        return remote(
+            ring.at[d, s, pair(g)], ring.at[d, s - 1, pair(g)],
             sr.at[d, s - 1, g], rr.at[d, s - 1, g], b_to[d],
         )
 
-    def z_up(g):
-        return remote(z_out.at[0, g], z_in.at[0, g], sz.at[0, g], rz.at[0, g], a_next)
-
-    def z_down(g):
-        return remote(z_out.at[1, g], z_in.at[1, g], sz.at[1, g], rz.at[1, g], a_prev)
-
-    def own_chunk(g, s):
-        to_partner(g, s).wait_recv()
-
-        @when(s < H - 1)
+    def z_send(j, to):
+        return remote(z_out.at[j], z_in.at[j], sz.at[j], rz.at[j], device(to % R, b))
+
+    def sum_step(k, g):
+        s = 2 * H + 1 - k + g
+
+        @when(s == H)
         def _():
             for d in range(2):
-                ring_r(d, s + 1, g, whole_z).wait_recv()
-
-        @when(s == H - 1)
-        def _():
-            ring_r(0, H, g, lows_z).wait_recv()
-            ring_r(1, H, g, highs_z).wait_recv()
-
-        pair = pl.ds(2 * g, 2)
-
-        @when(s >= 1)
-        def _():
-            lhs = jnp.concatenate(
-                [hid[(R - s) % R, pair].reshape(32, ff), hid[s, pair].reshape(32, ff)], axis=0
-            )
-
-            def cols(t, cc):
-                at = pl.ds(pl.multiple_of(t * C, 128), C)
-                p = jnp.dot(lhs, wdn[core, :, at], preferred_element_type=F32).reshape(2, 2, 16, C)
-                p = p + prx[g, s, :, :, :, at].astype(F32)
-                for d in range(2):
-                    ring[d, s, pair, :, at] = (p[d] + ring[d, s, pair, :, at].astype(F32)).astype(BF16)
+                ring_first(d, g).start()
+
+        @when((s >= 0) & (s < H))
+        def _():
+            for d in range(2):
+                @when(s == H - 1)
+                def _(d=d):
+                    ring_first(d, g).wait_recv()
+
+                @when(s < H - 1)
+                def _(d=d):
+                    ring_r(d, s + 1, g).wait_recv()
+
+                @when(s >= 1)
+                def _(d=d):
+                    ring[d, s, pair(g)] = (
+                        ring[d, s, pair(g)].astype(F32) + prx[g, s, d].astype(F32)
+                    ).astype(BF16)
+                    ring_r(d, s, g).start()
+
+        @when(s == 0)
+        def _():
+            v = ring[0, 0, pair(g)].astype(F32) + ring[1, 0, pair(g)].astype(F32)
+            v = v + prx[g, 0, 0].astype(F32)
+            z_out[pair(g)] = v.astype(BF16)
+
+            @when(g == 0)
+            def _():
+                fin[...] = v[0]
+
+            @when(g >= 1)
+            def _():
+                z_send(2 * g, a + R - g).start()
+
+            z_send(2 * g + 1, a + g + 1).start()
+
+    def over_groups(body):
+        lax.fori_loop(0, H, lambda g, c: (body(g), c)[1], 0)
+
+    def stage(k, c):
+        over_groups(lambda g: gather_step(k, g))
+        over_groups(lambda i: sum_step(k, H - 1 - i))
+
+        @when(k == 0)
+        def _():
+            for w in weights:
+                w.wait()
+
+        arrivals(k, own_arrivals)
+        arrivals(k, par_arrivals)
+        new = k - H
+
+        @when((new >= 0) & (new < H))
+        def _():
+            def near(n, cc):
+                activate(n, new)
                 return cc
 
-            lax.fori_loop(0, half // C, cols, 0)
-
-            @when(s < H)
-            def _():
-                for d in range(2):
-                    ring_r(d, s, g, whole_z).start()
-
-            @when(s == H)
-            def _():
-                ring_r(0, H, g, lows_z).start()
-                ring_r(1, H, g, highs_z).start()
-
-        @when(s == 0)
-        def _():
-            @when(g < H - 1)
-            def _():
-                z_up(g + 1).wait_recv()
-                z_down(g + 1).wait_recv()
-
-            lhs = hid[0, pair].reshape(32, ff)
-
-            def cols(t, cc):
-                at = pl.ds(pl.multiple_of(t * C, 128), C)
-                p = jnp.dot(lhs, wdn[core, :, at], preferred_element_type=F32).reshape(2, 16, C)
-                p = p + prx[g, 0, 0, :, :, at].astype(F32)
-                p = p + ring[0, 0, pair, :, at].astype(F32) + ring[1, 0, pair, :, at].astype(F32)
-                near = p[0] + z_in[1, g + 1, :, at].astype(F32)
-                far = p[1] + z_in[0, g + 1, :, at].astype(F32)
-                fin[:, at] = near
-                z_out[1, g, :, at] = near.astype(BF16)
-                z_out[0, g, :, at] = far.astype(BF16)
+            def rest(g, cc):
+                activate(new, g)
+                activate(R - 1 - new, g)
                 return cc
 
-            lax.fori_loop(0, half // C, cols, 0)
-            z_up(g).start()
-
-            @when(g >= 1)
-            def _():
-                z_down(g).start()
-
-    def sum_stage(k, c):
-        def own(i, cc):
-            s = H - (k - 1) + i
-
-            @when((s >= 0) & (s <= H) & (k >= 1))
-            def _():
-                own_chunk(H - 1 - i, s)
-
-            return cc
-
-        def other(i, cc):
-            s = H - k + i
+            lax.fori_loop(new, R - new, near, 0)
+            lax.fori_loop(new + 1, H, rest, 0)
+            partner_chunk(new, H)
+
+        def ahead(g):
+            s = H - (k - H - g)
+
+            @when((s >= 1) & (s <= H))
+            def _():
+                partner_chunk(g, s - 1)
+
+        def base(g):
+            s = H - (k - H - g)
 
             @when((s >= 0) & (s <= H))
             def _():
-                partner_chunk(H - 1 - i, s)
-
-            return cc
-
-        lax.fori_loop(0, H, own, 0)
-        lax.fori_loop(0, H, other, 0)
+                own_chunk(g, s)
+
+        over_groups(ahead)
+        over_groups(base)
         return c
 
-    lax.fori_loop(0, 2 * H + 1, sum_stage, 0)
-    z_up(0).wait_recv()
-
-    total = fin[...] + z_in[0, 0].astype(F32)
+    lax.fori_loop(0, 3 * H + 1, stage, 0)
+    bias_out[...] = bias_ref[...] + 2.0 / math.sqrt(average) * (average - loads[:, pl.ds(0, experts)])
+
+    total = fin[...]
+    for j in range(1, R):
+        z_send(j, a + 1).wait_recv()
+        total = total + z_in[j].astype(F32)
     f_out[...] = jnp.where(first, total[8:], total[:8])
     kept = jnp.where(first, total[:8], total[8:])
     last = remote(f_out, f_in, sf.at[0], sf.at[1], partner)
@@ -418,13 +437,13 @@
             def _():
                 ring_x(0, H - 1, g, lows).wait_send()
                 ring_x(1, H - 1, g, highs).wait_send()
-                ring_r(0, H, g, lows_z).wait_send()
-                ring_r(1, H, g, highs_z).wait_send()
+                for d in range(2):
+                    ring_first(d, g).wait_send()
 
             @when(s < H - 1)
             def _():
                 for d in range(2):
-                    ring_r(d, s + 1, g, whole_z).wait_send()
+                    ring_r(d, s + 1, g).wait_send()
 
             return cc
 
@@ -441,11 +460,11 @@
             return cc
 
         lax.fori_loop(0, H + 1, per_p, 0)
-        z_up(g).wait_send()
+        z_send(2 * g + 1, a + 1).wait_send()
 
         @when(g >= 1)
         def _():
-            z_down(g).wait_send()
+            z_send(2 * g, a + 1).wait_send()
 
         return c
 
@@ -487,15 +506,17 @@
             pltpu.VMEM((2, half, 2 * ff), BF16),
             pltpu.VMEM((2, ff, half), BF16),
             pltpu.VMEM((R, R, 16, 2 * ff), F32),
+            pltpu.VMEM((R, R, 16, 2 * ff), F32),
             pltpu.VMEM((R, R, 16, ff), BF16),
             pltpu.VMEM((H, H + 1, 2, 2, 16, half), BF16),
             pltpu.VMEM((H, H + 1, 2, 2, 16, half), BF16),
-            pltpu.VMEM((2, H + 1, R, 16, half), BF16),
-            pltpu.VMEM((2, H, 16, half), BF16),
-            pltpu.VMEM((2, H + 1, 16, half), BF16),
+            pltpu.VMEM((2, H, R, 16, half), BF16),
+            pltpu.VMEM((R, 16, half), BF16),
+            pltpu.VMEM((R, 16, half), BF16),
             pltpu.VMEM((16, half), F32),
             pltpu.VMEM((tok_rows, half), F32),
             pltpu.VMEM((tok_rows, half), F32),
+            pltpu.VMEM((1, 128), F32),
             dma((6,)),
             dma((2,)),
             dma((2, H)),
@@ -508,8 +529,8 @@
             dma((H, H + 1)),
             dma((2, H, H)),
             dma((2, H, H)),
-            dma((2, H)),
-            dma((2, H)),
+            dma((R,)),
+            dma((R,)),
             dma((2,)),
         ],
         compiler_params=pltpu.CompilerParams(

time: 155 us -> 140 us (0.903)
  Pallas kernels: 152 us -> 136 us
    pallas_call x1, Pallas kernels: 152 us -> 136 us  [per_device(): pl.pallas_call(functools.partial(kernel, (side, count, shards, average)),...]
where the time goes in v3:
time: 140 us; the launch traced here: 139 us
  Pallas kernels  136 us (97%)
  local copies, waits for them, and re-layouts  2.66 us (2%)
    pallas_call x1, Pallas kernels, per_device(): pl.pallas_call(functools.partial(kernel, (side, count, shards, average)),...  136 us

profile of v3, /device:TPU:513, one launch (start us, length us, event | category | flops | bytes accessed | tf_op | source)
XLA Modules:
  0.0 139.4 jit_solution(5685125422543311564)
XLA Ops:
  0.6 136.1 %routed_experts.1 = (bf16[8,7168]{1,0:T(8,128)(2,1)}, f32[1,16]{1,0:T(1,128)}) custom-call(s32[8]{0:T(128)} %home.1, bf16[8,7168]{1,0:T(8,128)(2,1)} %tok.1, s32[8,8]{1,0:T(8,128)} %exp_ref.1, s32[8,8]{1,0:T(8,128)} %gate_ref.1, f32[1,16]{1,0:T(1,128)} %bitcast.2, bf16[7168,256]{1,0:T(8,128)(2,1)} %wg.1, bf16[7168,256]{1,0:T(8,128)(2,1)} %wu.1, ...), custom_call_target="tpu_custom_call" | custom-call | tf_op jit(solution)/shard_map/routed_experts/pallas_call | solution.py:493
  136.7 1.6 %copy.12 = bf16[8,7168]{1,0:T(8,128)(2,1)} copy(bf16[8,7168]{1,0:T(8,128)(2,1)} %get-tuple-element.8) | data formatting | bytes 229376
  138.2 1.1 copy.13

commit v4 on v3

--- a/solution.py
+++ b/solution.py
@@ -25,6 +25,7 @@
 ):
     side, experts, shards, average = dims
     R, H = side, side // 2
+    assert R == 8
     top = exp_ref.shape[1]
     half = tok.shape[1] // 2
     wide = half + 128
@@ -63,7 +64,7 @@
         w.start()
 
     barrier = pltpu.get_barrier_semaphore()
-    for to in [partner, b_next, b_prev] + [device((a + i) % R, b) for i in range(1, R)]:
+    for to in [partner, b_next, b_prev] + [device((a + i) % R, b) for i in (1, 2, R - 2, R - 1)]:
         pl.semaphore_signal(barrier, inc=1, device_id=to, device_id_type=pl.DeviceIdType.MESH)
 
     fixed = gate_ref[...].astype(F32)
@@ -93,7 +94,7 @@
     xs[:, pl.ds(0, half)] = jnp.where(first, hi_half, lo_half).astype(BF16)
     xs[:, pl.ds(half, 128)] = meta.astype(BF16)
 
-    pl.semaphore_wait(barrier, R + 2)
+    pl.semaphore_wait(barrier, 7)
     swap = remote(xs, xr, x_sem.at[0], x_sem.at[1], partner)
     swap.start()
     swap.wait_recv()
@@ -255,52 +256,68 @@
     def to_partner(g, s):
         return remote(pst.at[g, s], prx.at[g, s], sp.at[g, s], rp.at[g, s], partner)
 
-    def partner_chunk(g, s):
-        j1, j2 = slot_of((R - s) % R), slot_of(s)
-        lhs = jnp.concatenate(
-            [hid[g, j1], hid[R - 1 - g, j1], hid[g, j2], hid[R - 1 - g, j2]], axis=0
-        )
-
-        def cols(t, cc):
+    def partner_chunks(chunks):
+        lhs = []
+        for g, s in chunks:
+            j1, j2 = slot_of((R - s) % R), slot_of(s)
+            lhs += [hid[g, j1], hid[R - 1 - g, j1], hid[g, j2], hid[R - 1 - g, j2]]
+        lhs = jnp.concatenate(lhs, axis=0)
+        for t in range(half // C):
             at = pl.ds(t * C, C)
-            p = jnp.dot(lhs, wdn[1 - core, :, at], preferred_element_type=F32)
-            pst[g, s, :, :, :, at] = p.astype(BF16).reshape(2, 2, 16, C)
-            return cc
-
+            p = jnp.dot(lhs, wdn[1 - core, :, at], preferred_element_type=F32).astype(BF16)
+            for i, (g, s) in enumerate(chunks):
+                pst[g, s, :, :, :, at] = p[64 * i : 64 * i + 64].reshape(2, 2, 16, C)
+        for g, s in chunks:
+            to_partner(g, s).start()
+
+    def own_chunks(chunks):
+        lhs = []
+        for g, s in chunks:
+            lhs += [hid[n, pair(g)].reshape(32, ff) for n in ((R - s) % R, s)]
+            to_partner(g, s).wait_recv()
+        lhs = jnp.concatenate(lhs, axis=0)
         for t in range(half // C):
-            cols(t, 0)
-        to_partner(g, s).start()
-
-    def own_chunk(g, s):
-        lhs = jnp.concatenate(
-            [hid[(R - s) % R, pair(g)].reshape(32, ff), hid[s, pair(g)].reshape(32, ff)], axis=0
-        )
-        to_partner(g, s).wait_recv()
-
-        def cols(t, cc):
             at = pl.ds(t * C, C)
-            p = jnp.dot(lhs, wdn[core, :, at], preferred_element_type=F32).reshape(2, 2, 16, C)
-            prx[g, s, :, :, :, at] = (p + prx[g, s, :, :, :, at].astype(F32)).astype(BF16)
-            return cc
-
-        for t in range(half // C):
-            cols(t, 0)
+            p = jnp.dot(lhs, wdn[core, :, at], preferred_element_type=F32)
+            for i, (g, s) in enumerate(chunks):
+                mine = p[64 * i : 64 * i + 64].reshape(2, 2, 16, C)
+                prx[g, s, :, :, :, at] = (mine + prx[g, s, :, :, :, at].astype(F32)).astype(BF16)
+
+    def in_pairs(lo, hi, body):
+        count = jnp.maximum(hi - lo, 0)
+
+        def two(i, c):
+            body([lo + 2 * i, lo + 2 * i + 1])
+            return c
+
+        lax.fori_loop(0, count // 2, two, 0)
+
+        @when(count % 2 == 1)
+        def _():
+            body([hi - 1])
 
     whole_z = pl.ds(0, half)
     lows_z, highs_z = pl.ds(0, cut), pl.ds(cut, half - cut)
 
+    halves_z = (lows_z, highs_z)
+
     def ring_first(d, g):
-        cols = highs_z if d else lows_z
+        cols = halves_z[d]
         return remote(
             prx.at[g, H, d, :, :, cols], ring.at[d, H - 1, pair(g), :, cols],
-            sr.at[d, H - 1, g], rr.at[d, H - 1, g], b_to[d],
-        )
-
-    def ring_r(d, s, g):
+            sr.at[d, H - 1, g, d], rr.at[d, H - 1, g, d], b_to[d],
+        )
+
+    def ring_r(d, s, g, h):
+        cols = halves_z[h]
         return remote(
-            ring.at[d, s, pair(g)], ring.at[d, s - 1, pair(g)],
-            sr.at[d, s - 1, g], rr.at[d, s - 1, g], b_to[d],
-        )
+            ring.at[d, s, pair(g), :, cols], ring.at[d, s - 1, pair(g), :, cols],
+            sr.at[d, s - 1, g, h], rr.at[d, s - 1, g, h], b_to[d],
+        )
+
+    def arrived(d, s, g, h):
+        here = ring.at[d, s, pair(g), :, halves_z[h]]
+        remote(here, here, sr.at[d, s, g, h], rr.at[d, s, g, h], b_to[d]).wait_recv()
 
     def z_send(j, to):
         return remote(z_out.at[j], z_in.at[j], sz.at[j], rz.at[j], device(to % R, b))
@@ -313,39 +330,54 @@
             for d in range(2):
                 ring_first(d, g).start()
 
-        @when((s >= 0) & (s < H))
-        def _():
+        @when((s >= 1) & (s < H))
+        def _():
+            for h in range(2):
+                for d in range(2):
+                    cols = halves_z[h]
+                    if h == d:
+                        arrived(d, s, g, h)
+                    else:
+                        @when(s < H - 1)
+                        def _(d=d, h=h):
+                            arrived(d, s, g, h)
+
+                    ring[d, s, pair(g), :, cols] = (
+                        ring[d, s, pair(g), :, cols].astype(F32) + prx[g, s, d, :, :, cols].astype(F32)
+                    ).astype(BF16)
+                    ring_r(d, s, g, h).start()
+
+    def last_sum(g):
+        for h in range(2):
             for d in range(2):
-                @when(s == H - 1)
-                def _(d=d):
-                    ring_first(d, g).wait_recv()
-
-                @when(s < H - 1)
-                def _(d=d):
-                    ring_r(d, s + 1, g).wait_recv()
-
-                @when(s >= 1)
-                def _(d=d):
-                    ring[d, s, pair(g)] = (
-                        ring[d, s, pair(g)].astype(F32) + prx[g, s, d].astype(F32)
-                    ).astype(BF16)
-                    ring_r(d, s, g).start()
-
-        @when(s == 0)
-        def _():
-            v = ring[0, 0, pair(g)].astype(F32) + ring[1, 0, pair(g)].astype(F32)
-            v = v + prx[g, 0, 0].astype(F32)
-            z_out[pair(g)] = v.astype(BF16)
-
-            @when(g == 0)
-            def _():
-                fin[...] = v[0]
-
-            @when(g >= 1)
-            def _():
-                z_send(2 * g, a + R - g).start()
-
-            z_send(2 * g + 1, a + g + 1).start()
+                arrived(d, 0, g, h)
+
+        def part_of(i):
+            v = ring[0, 0, 2 * g + i].astype(F32) + ring[1, 0, 2 * g + i].astype(F32)
+            v = v + prx[g, 0, 0, i].astype(F32)
+            z_out[2 * g + i] = v.astype(BF16)
+            return v
+
+        part_of(1)
+
+        @when(g >= 2)
+        def _():
+            z_send(2 * g + 1, a + 2).start()
+
+        near = part_of(0)
+
+        @when(g >= 2)
+        def _():
+            z_send(2 * g, a + R - 2).start()
+
+        @when(g == 0)
+        def _():
+            fin[...] = near
+
+    def pass_on(held, far, step):
+        z_send(far, a + 2).wait_recv()
+        z_out[held] = (z_out[held].astype(F32) + z_in[far].astype(F32)).astype(BF16)
+        z_send(held, a + step).start()
 
     def over_groups(body):
         lax.fori_loop(0, H, lambda g, c: (body(g), c)[1], 0)
@@ -376,32 +408,79 @@
 
             lax.fori_loop(new, R - new, near, 0)
             lax.fori_loop(new + 1, H, rest, 0)
-            partner_chunk(new, H)
-
-        def ahead(g):
-            s = H - (k - H - g)
-
-            @when((s >= 1) & (s <= H))
-            def _():
-                partner_chunk(g, s - 1)
-
-        def base(g):
-            s = H - (k - H - g)
-
-            @when((s >= 0) & (s <= H))
-            def _():
-                own_chunk(g, s)
-
-        over_groups(ahead)
-        over_groups(base)
+            partner_chunks([(new, H), (new, H - 1)])
+
+        in_pairs(
+            jnp.maximum(new - H + 1, 0), jnp.minimum(new, H),
+            lambda gs: partner_chunks([(g, H - 1 - new + g) for g in gs]),
+        )
+        in_pairs(
+            jnp.maximum(new - H, 0), jnp.minimum(new + 1, H),
+            lambda gs: own_chunks([(g, H - new + g) for g in gs]),
+        )
+
+        @when(k >= 2 * H + 1)
+        def _():
+            last_sum(k - (2 * H + 1))
+
         return c
 
     lax.fori_loop(0, 3 * H + 1, stage, 0)
     bias_out[...] = bias_ref[...] + 2.0 / math.sqrt(average) * (average - loads[:, pl.ds(0, experts)])
 
+    swap.wait_send()
+
+    def drain_g(g, c):
+        down(g).wait_send()
+
+        @when(g < H - 1)
+        def _():
+            up(g).wait_send()
+
+        def per_s(s, cc):
+            @when(s < H - 1)
+            def _():
+                for d in range(2):
+                    ring_x(d, s, g, whole).wait_send()
+
+            @when(s == H - 1)
+            def _():
+                ring_x(0, H - 1, g, lows).wait_send()
+                ring_x(1, H - 1, g, highs).wait_send()
+                for d in range(2):
+                    ring_first(d, g).wait_send()
+
+            @when(s < H - 1)
+            def _():
+                for d in range(2):
+                    for h in range(2):
+                        ring_r(d, s + 1, g, h).wait_send()
+
+            return cc
+
+        lax.fori_loop(0, H, per_s, 0)
+
+        def per_n(n, cc):
+            across(n, g).wait_send()
+            return cc
+
+        lax.fori_loop(0, R, per_n, 0)
+
+        def per_p(s, cc):
+            to_partner(g, s).wait_send()
+            return cc
+
+        lax.fori_loop(0, H + 1, per_p, 0)
+        return c
+
+    lax.fori_loop(0, H, drain_g, 0)
+
+    pass_on(1, 5, 1)
+    pass_on(3, 7, 2)
+    pass_on(2, 6, R - 1)
     total = fin[...]
-    for j in range(1, R):
-        z_send(j, a + 1).wait_recv()
+    for j in (4, 1, 2, 3):
+        z_send(j, a + 2).wait_recv()
         total = total + z_in[j].astype(F32)
     f_out[...] = jnp.where(first, total[8:], total[:8])
     kept = jnp.where(first, total[:8], total[8:])
@@ -418,58 +497,8 @@
 
     kept = place(kept)
 
-    swap.wait_send()
-
-    def drain_g(g, c):
-        down(g).wait_send()
-
-        @when(g < H - 1)
-        def _():
-            up(g).wait_send()
-
-        def per_s(s, cc):
-            @when(s < H - 1)
-            def _():
-                for d in range(2):
-                    ring_x(d, s, g, whole).wait_send()
-
-            @when(s == H - 1)
-            def _():
-                ring_x(0, H - 1, g, lows).wait_send()
-                ring_x(1, H - 1, g, highs).wait_send()
-                for d in range(2):
-                    ring_first(d, g).wait_send()
-
-            @when(s < H - 1)
-            def _():
-                for d in range(2):
-                    ring_r(d, s + 1, g).wait_send()
-
-            return cc
-
-        lax.fori_loop(0, H, per_s, 0)
-
-        def per_n(n, cc):
-            across(n, g).wait_send()
-            return cc
-
-        lax.fori_loop(0, R, per_n, 0)
-
-        def per_p(s, cc):
-            to_partner(g, s).wait_send()
-            return cc
-
-        lax.fori_loop(0, H + 1, per_p, 0)
-        z_send(2 * g + 1, a + 1).wait_send()
-
-        @when(g >= 1)
-        def _():
-            z_send(2 * g, a + 1).wait_send()
-
-        return c
-
-    lax.fori_loop(0, H, drain_g, 0)
-
+    for j in range(1, R):
+        z_send(j, a + 2).wait_send()
     last.wait()
     other = place(f_in[...])
     out[:, pl.ds(0, half)] = jnp.where(first, kept, other).astype(BF16)
@@ -527,8 +556,8 @@
             dma((R, H)),
             dma((H, H + 1)),
             dma((H, H + 1)),
-            dma((2, H, H)),
-            dma((2, H, H)),
+            dma((2, H, H, 2)),
+            dma((2, H, H, 2)),
             dma((R,)),
             dma((R,)),
             dma((2,)),

time: 140 us -> 131 us (0.936)
  Pallas kernels: 136 us -> 127 us
    pallas_call x1, Pallas kernels: 136 us -> 127 us  [per_device(): pl.pallas_call(functools.partial(kernel, (side, count, shards, average)),...]
where the time goes in v4:
time: 131 us
  Pallas kernels  127 us (97%)
  local copies, waits for them, and re-layouts  2.66 us (2%)
    pallas_call x1, Pallas kernels, per_device(): pl.pallas_call(functools.partial(kernel, (side, count, shards, average)),...  127 us
    unnamed x2, local copies, waits for them, and re-layouts  2.66 us

profile of v4, /device:TPU:513, one launch (start us, length us, event | category | flops | bytes accessed | tf_op | source)
XLA Modules:
  0.0 130.7 jit_solution(9052043733331728462)
XLA Ops:
  0.6 127.4 %routed_experts.1 = (bf16[8,7168]{1,0:T(8,128)(2,1)}, f32[1,16]{1,0:T(1,128)}) custom-call(s32[8]{0:T(128)} %home.1, bf16[8,7168]{1,0:T(8,128)(2,1)} %tok.1, s32[8,8]{1,0:T(8,128)} %exp_ref.1, s32[8,8]{1,0:T(8,128)} %gate_ref.1, f32[1,16]{1,0:T(1,128)} %bitcast.2, bf16[7168,256]{1,0:T(8,128)(2,1)} %wg.1, bf16[7168,256]{1,0:T(8,128)(2,1)} %wu.1, ...), custom_call_target="tpu_custom_call" | custom-call | tf_op jit(solution)/shard_map/routed_experts/pallas_call | solution.py:522
  128.1 1.6 %copy.12 = bf16[8,7168]{1,0:T(8,128)(2,1)} copy(bf16[8,7168]{1,0:T(8,128)(2,1)} %get-tuple-element.8) | data formatting | bytes 229376
  129.6 1.1 copy.13

commit v5 on v4

--- a/solution.py
+++ b/solution.py
@@ -88,8 +88,17 @@
     meta = jnp.where(part == 2, mid, meta)
     meta = jnp.where(part == 3, low, meta)
     first = core == 0
-    lo_half = tok[:, pl.ds(0, half)].astype(F32)
-    hi_half = tok[:, pl.ds(half, half)].astype(F32)
+
+    def place(v):
+        row = lax.broadcasted_iota(jnp.int32, v.shape, 0)
+        placed = jnp.zeros(v.shape, F32)
+        for t in range(v.shape[0]):
+            placed = jnp.where(row == home[t], jnp.broadcast_to(v[t : t + 1], v.shape), placed)
+        return placed
+
+    meta = place(meta)
+    lo_half = place(tok[:, pl.ds(0, half)].astype(F32))
+    hi_half = place(tok[:, pl.ds(half, half)].astype(F32))
     mine = jnp.where(first, lo_half, hi_half)
     xs[:, pl.ds(0, half)] = jnp.where(first, hi_half, lo_half).astype(BF16)
     xs[:, pl.ds(half, 128)] = meta.astype(BF16)
@@ -305,19 +314,14 @@
         cols = halves_z[d]
         return remote(
             prx.at[g, H, d, :, :, cols], ring.at[d, H - 1, pair(g), :, cols],
-            sr.at[d, H - 1, g, d], rr.at[d, H - 1, g, d], b_to[d],
-        )
-
-    def ring_r(d, s, g, h):
-        cols = halves_z[h]
+            sr.at[d, H - 1, g], rr.at[d, H - 1, g], b_to[d],
+        )
+
+    def ring_r(d, s, g):
         return remote(
-            ring.at[d, s, pair(g), :, cols], ring.at[d, s - 1, pair(g), :, cols],
-            sr.at[d, s - 1, g, h], rr.at[d, s - 1, g, h], b_to[d],
-        )
-
-    def arrived(d, s, g, h):
-        here = ring.at[d, s, pair(g), :, halves_z[h]]
-        remote(here, here, sr.at[d, s, g, h], rr.at[d, s, g, h], b_to[d]).wait_recv()
+            ring.at[d, s, pair(g)], ring.at[d, s - 1, pair(g)],
+            sr.at[d, s - 1, g], rr.at[d, s - 1, g], b_to[d],
+        )
 
     def z_send(j, to):
         return remote(z_out.at[j], z_in.at[j], sz.at[j], rz.at[j], device(to % R, b))
@@ -332,25 +336,23 @@
 
         @when((s >= 1) & (s < H))
         def _():
-            for h in range(2):
-                for d in range(2):
-                    cols = halves_z[h]
-                    if h == d:
-                        arrived(d, s, g, h)
-                    else:
-                        @when(s < H - 1)
-                        def _(d=d, h=h):
-                            arrived(d, s, g, h)
-
-                    ring[d, s, pair(g), :, cols] = (
-                        ring[d, s, pair(g), :, cols].astype(F32) + prx[g, s, d, :, :, cols].astype(F32)
-                    ).astype(BF16)
-                    ring_r(d, s, g, h).start()
+            for d in range(2):
+                @when(s == H - 1)
+                def _(d=d):
+                    ring_first(d, g).wait_recv()
+
+                @when(s < H - 1)
+                def _(d=d):
+                    ring_r(d, s + 1, g).wait_recv()
+
+                ring[d, s, pair(g)] = (
+                    ring[d, s, pair(g)].astype(F32) + prx[g, s, d].astype(F32)
+                ).astype(BF16)
+                ring_r(d, s, g).start()
 
     def last_sum(g):
-        for h in range(2):
-            for d in range(2):
-                arrived(d, 0, g, h)
+        for d in range(2):
+            ring_r(d, 1, g).wait_recv()
 
         def part_of(i):
             v = ring[0, 0, 2 * g + i].astype(F32) + ring[1, 0, 2 * g + i].astype(F32)
@@ -453,8 +455,7 @@
             @when(s < H - 1)
             def _():
                 for d in range(2):
-                    for h in range(2):
-                        ring_r(d, s + 1, g, h).wait_send()
+                    ring_r(d, s + 1, g).wait_send()
 
             return cc
 
@@ -482,25 +483,14 @@
     for j in (4, 1, 2, 3):
         z_send(j, a + 2).wait_recv()
         total = total + z_in[j].astype(F32)
-    f_out[...] = jnp.where(first, total[8:], total[:8])
+    f_out[...] = jnp.where(first, total[8:], total[:8]).astype(BF16)
     kept = jnp.where(first, total[:8], total[8:])
     last = remote(f_out, f_in, sf.at[0], sf.at[1], partner)
     last.start()
-    row = lax.broadcasted_iota(jnp.int32, (8, half), 0)
-
-    def place(v):
-        v = v.astype(BF16).astype(F32)
-        placed = jnp.zeros((8, half), F32)
-        for t in range(8):
-            placed = jnp.where(row == home[t], jnp.broadcast_to(v[t : t + 1], (8, half)), placed)
-        return placed
-
-    kept = place(kept)
-
     for j in range(1, R):
         z_send(j, a + 2).wait_send()
     last.wait()
-    other = place(f_in[...])
+    other = f_in[...].astype(F32)
     out[:, pl.ds(0, half)] = jnp.where(first, kept, other).astype(BF16)
     out[:, pl.ds(half, half)] = jnp.where(first, other, kept).astype(BF16)
 
@@ -543,8 +533,8 @@
             pltpu.VMEM((R, 16, half), BF16),
             pltpu.VMEM((R, 16, half), BF16),
             pltpu.VMEM((16, half), F32),
-            pltpu.VMEM((tok_rows, half), F32),
-            pltpu.VMEM((tok_rows, half), F32),
+            pltpu.VMEM((tok_rows, half), BF16),
+            pltpu.VMEM((tok_rows, half), BF16),
             pltpu.VMEM((1, 128), F32),
             dma((6,)),
             dma((2,)),
@@ -556,8 +546,8 @@
             dma((R, H)),
             dma((H, H + 1)),
             dma((H, H + 1)),
-            dma((2, H, H, 2)),
-            dma((2, H, H, 2)),
+            dma((2, H, H)),
+            dma((2, H, H)),
             dma((R,)),
             dma((R,)),
             dma((2,)),

time: 131 us -> 133 us (1.015)
  Pallas kernels: 127 us -> 129 us
    pallas_call x1, Pallas kernels: 127 us -> 129 us  [per_device(): pl.pallas_call(functools.partial(kernel, (side, count, shards, average)),...]
where the time goes in v5:
time: 133 us; the launch traced here: 132 us
  Pallas kernels  129 us (97%)
  local copies, waits for them, and re-layouts  2.66 us (2%)
    pallas_call x1, Pallas kernels, per_device(): pl.pallas_call(functools.partial(kernel, (side, count, shards, average)),...  129 us

profile of v5, /device:TPU:513, one launch (start us, length us, event | category | flops | bytes accessed | tf_op | source)
XLA Modules:
  0.0 132.4 jit_solution(886177868820890666)
XLA Ops:
  0.6 129.1 %routed_experts.1 = (bf16[8,7168]{1,0:T(8,128)(2,1)}, f32[1,16]{1,0:T(1,128)}) custom-call(s32[8]{0:T(128)} %home.1, bf16[8,7168]{1,0:T(8,128)(2,1)} %tok.1, s32[8,8]{1,0:T(8,128)} %exp_ref.1, s32[8,8]{1,0:T(8,128)} %gate_ref.1, f32[1,16]{1,0:T(1,128)} %bitcast.2, bf16[7168,256]{1,0:T(8,128)(2,1)} %wg.1, bf16[7168,256]{1,0:T(8,128)(2,1)} %wu.1, ...), custom_call_target="tpu_custom_call" | custom-call | tf_op jit(solution)/shard_map/routed_experts/pallas_call | solution.py:512
  129.8 1.6 %copy.12 = bf16[8,7168]{1,0:T(8,128)(2,1)} copy(bf16[8,7168]{1,0:T(8,128)(2,1)} %get-tuple-element.8) | data formatting | bytes 229376
  131.3 1.1 copy.13
